TPU v7x, 512 devices: a whole 4x4x16 slice. The times are simulated.
512 devices in a mesh: dp: 4 (over x), expert: 128 (over y, z, core).
Axes of the slice: x: 4, y: 4, z: 16, core: 2. Of those that a mesh axis runs over, the one named last changes fastest.
Arguments:
- tokens: bfloat16 [49152, 2048], P(('dp', 'expert')), may hold values from -6 to 6
- routes: int32 [49152, 8], P(('dp', 'expert')), may hold values from 0 to 127, all different within a row; in each aligned block of 96 rows (0 to 95, 96 to 191, ...) at most 8 rows name the same one
- weights: bfloat16 [128, 2, 768, 2048], P('expert', None, 'dp'), may hold values from -0.125 to 0.125
- keep_mask: int32 [128, 2, 768, 128], P('expert', None, 'dp'), may hold values from 0 to 1, as said below
- inv_factor: float32 [128, 128, 2048], P('expert'), as said below
Outputs:
- hidden: bfloat16 [49152, 8, 768], P(('dp', 'expert'))
Inputs may be any that keep to these rules, and one draw needn't show every extreme that they name: `routes`: each token names 8 different experts; the 96 rows of one device name any one expert at most 8 times. `keep_mask`: each row of 128 entries holds exactly 64 ones. `inv_factor`: each expert's factor is upper triangular: entry (i, j) is zero for j < i, and the diagonal entry (i, i) lies in [0.6, 1.6].
All inputs are finite; a program needn't handle non-finite values.
Results may differ from a plain program's by a relative error of at most 0.0058.
Values may be sent and summed in bfloat16 or wider, within the bound.
A program may use at most 64 MiB of HBM per device.

v0:
```python
import jax
import jax.numpy as jnp
from jax import lax
from jax.sharding import PartitionSpec as P


def in_one_piece(arrays, axis, dim, along):
    both = jnp.concatenate(arrays, axis=along)
    filled, at, outs = (lax.all_gather(both, axis, axis=dim, tiled=True), 0, [])
    for a in arrays:
        outs.append(lax.slice_in_dim(filled, at, at + a.shape[along], axis=along))
        at += a.shape[along]
    return tuple(outs)


def prune_rows(weights, keep_mask, inv_factor):
    block_width = keep_mask.shape[-1]
    initial = weights.astype(jnp.float32)
    leading = initial[..., :block_width]
    dropped = (1 - keep_mask).astype(jnp.float32)
    factor_block = inv_factor[:, :, :block_width]

    def column(column_id, state):
        leading, errors = state
        current = lax.dynamic_index_in_dim(leading, column_id, 3, keepdims=False)
        factor_row = lax.dynamic_index_in_dim(factor_block, column_id, 1, keepdims=False)
        diagonal = lax.dynamic_index_in_dim(factor_row, column_id, 1, keepdims=False)
        error_col = (
            lax.dynamic_index_in_dim(dropped, column_id, 3, keepdims=False)
            * current
            / diagonal[:, None, None]
        )
        leading = leading - error_col[..., None] * factor_row[:, None, None, :]
        errors = lax.dynamic_update_index_in_dim(errors, error_col, column_id, 3)
        return (leading, errors)

    leading, errors = lax.fori_loop(0, block_width, column, (leading, jnp.zeros_like(leading)))
    trailing = initial[..., block_width:] - jnp.einsum(
        "epri,eij->eprj", errors, inv_factor[:, :, block_width:], precision=lax.Precision.HIGHEST
    )
    return jnp.concatenate([leading, trailing], axis=-1).astype(jnp.bfloat16)


def local(tokens, routes, weights, keep_mask, inv_factor):
    pruned = prune_rows(weights, keep_mask, inv_factor)
    gate_all, up_all = in_one_piece((pruned[0, 0], pruned[0, 1]), "dp", 0, 1)
    owners = lax.axis_size("expert")
    token_rows = tokens.shape[0]
    top_count = routes.shape[1]
    model_width = tokens.shape[1]
    capacity = token_rows * top_count * 4 // (3 * owners)
    slot_expert = routes.reshape(-1)
    one_hot = (slot_expert[:, None] == jnp.arange(owners, dtype=jnp.int32)[None, :]).astype(
        jnp.int32
    )
    slot_rank = jnp.sum(jnp.cumsum(one_hot, axis=0) * one_hot, axis=1) - 1
    target = slot_expert * capacity + slot_rank
    source = jnp.arange(slot_expert.shape[0], dtype=jnp.int32) // top_count
    outbox = (
        jnp.zeros((owners * capacity, model_width), jnp.bfloat16).at[target].set(tokens[source])
    )
    outbox = outbox.reshape(owners, capacity, model_width)
    arrived = lax.all_to_all(outbox, "expert", split_axis=0, concat_axis=0, tiled=True)
    arrived_rows = arrived.reshape(-1, model_width)
    gate_out = lax.dot_general(
        arrived_rows, gate_all, (((1,), (1,)), ((), ())), preferred_element_type=jnp.float32
    )
    up_out = lax.dot_general(
        arrived_rows, up_all, (((1,), (1,)), ((), ())), preferred_element_type=jnp.float32
    )
    hidden_rows = (jax.nn.silu(gate_out) * up_out).astype(jnp.bfloat16)
    hidden_rows = hidden_rows.reshape(arrived.shape[0], arrived.shape[1], -1)
    results = lax.all_to_all(hidden_rows, "expert", split_axis=0, concat_axis=0, tiled=True)
    hidden = results.reshape(owners * capacity, -1)[target]
    return hidden.reshape(token_rows, top_count, -1)


def solution(mesh):
    return jax.shard_map(
        local,
        mesh=mesh,
        in_specs=(
            P(("dp", "expert"), None),
            P(("dp", "expert"), None),
            P("expert", None, "dp", None),
            P("expert", None, "dp", None),
            P("expert", None, None),
        ),
        out_specs=P(("dp", "expert"), None, None),
        check_vma=False,
    )
```

profile of v0, /device:TPU:1, one launch (start us, length us, event | category | flops | bytes accessed | tf_op | source)
XLA Modules:
  0.0 481.6 jit_solution(8317621784662831519)
XLA Ops:
  6.6 0.7 broadcast_multiply_fusion
  7.3 0.8 copy.7
  9.3 23.0 %scatter_custom_fusion = bf16[1024,2048]{1,0:T(8,128)(2,1)} fusion(s32[768]{0:T(1024)S(1)} %fusion.30, bf16[96,2048]{1,0:T(8,128)(2,1)S(1)} %copy-done, s32[1024]{0:T(1024)S(1)} %pad_clamp_fusion.1, bf16[]{:T(256)} %constant.139.clone.1), kind=kCustom, calls=%fused_computation.15 | custom fusion | bytes 4194306 | tf_op jit(solution)/shard_map/scatter | solution.py:60
  32.3 21.1 %all-to-all-start = ((bf16[128,8,2048]{2,1,0:T(8,128)(2,1)}), bf16[128,8,2048]{2,1,0:T(8,128)(2,1)}, u32[]{:S(2)}, u32[]{:S(2)}) async-start(bf16[128,8,2048]{2,1,0:T(8,128)(2,1)} %bitcast.48), calls=%async_computation | async-start | bytes 8388608 | tf_op jit(solution)/shard_map/all_to_all | solution.py:63
  54.0 228.4 %while.18 = (s32[]{:T(128)}, f32[1,2,192,128]{2,1,3,0:T(2,128)S(1)}, f32[1,2,192,128]{2,1,3,0:T(2,128)S(1)}, f32[1,2,192,128]{2,1,3,0:T(2,128)S(1)}, f32[1,128,1...) while((s32[]{:T(128)}, f32[1,2,192,128]{2,1,3,0:T(2,128)S(1)}, f32[1,2,192,128]{2,1,3,0:T(2,128)S(1)}, ...), condition=%wide.region_5.6_spmd, body=%wide.region_4.5_spmd.sunk | while | flops 99075 | bytes 404613 | solution.py:37
  55.2 0.6 multiply_subtract_fusion.2
  58.7 0.6 multiply_subtract_fusion.2
  62.3 0.6 multiply_subtract_fusion.2
  65.9 0.6 multiply_subtract_fusion.2
  67.6 0.6 multiply_subtract_fusion.2
  69.4 0.6 multiply_subtract_fusion.2
  71.2 0.6 multiply_subtract_fusion.2
  73.0 0.6 multiply_subtract_fusion.2
  74.8 0.6 multiply_subtract_fusion.2
  78.3 0.6 multiply_subtract_fusion.2
  81.9 0.6 multiply_subtract_fusion.2
  85.5 0.6 multiply_subtract_fusion.2
  89.1 0.6 multiply_subtract_fusion.2
  92.6 0.6 multiply_subtract_fusion.2
  96.2 0.6 multiply_subtract_fusion.2
  99.8 0.6 multiply_subtract_fusion.2
  101.5 0.6 multiply_subtract_fusion.2
  103.3 0.6 multiply_subtract_fusion.2
  282.4 2.0 convert_element_type.24
  284.5 4.1 fusion.9
  288.9 1.3 pad_maximum_fusion
  290.2 74.2 %all-gather.2.cloned.1.call-done = bf16[768,4096]{1,0:T(8,128)(2,1)} async-done(((bf16[192,4096]{1,0:T(8,128)(2,1)}), bf16[768,4096]{1,0:T(8,128)(2,1)}) %all-gather.2.cloned.1.call-update) | async-done | bytes 6291472 | tf_op jit(solution)/shard_map/all_gather | solution.py:9
  364.4 6.4 %fusion.3 = f32[1024,768]{1,0:T(8,128)S(1)} fusion(bf16[128,8,2048]{2,1,0:T(8,128)(2,1)} %all-to-all-done, bf16[768,4096]{1,0:T(8,128)(2,1)} %all-gather.2.cloned.1.call-done), kind=kOutput, calls=%fused_computation.11 | convolution fusion | flops 3221225472 | bytes 10485760 | tf_op jit(solution)/shard_map/dot_general | solution.py:65
  370.8 7.1 %fusion.15 = bf16[128,8,768]{2,1,0:T(8,128)(2,1)} fusion(bf16[768,4096]{1,0:T(8,128)(2,1)S(1)} %copy-done.4, bf16[128,8,2048]{2,1,0:T(8,128)(2,1)} %all-to-all-done, f32[1024,768]{1,0:T(8,128)S(1)} %fusion.3), kind=kOutput, calls=%fused_computation.25 | convolution fusion | flops 3225944064 | bytes 12058624 | tf_op jit(solution)/shard_map/dot_general | solution.py:68
  377.9 16.8 %all-to-all-start.1 = ((bf16[128,8,768]{2,1,0:T(8,128)(2,1)}), bf16[128,8,768]{2,1,0:T(8,128)(2,1)S(1)}, u32[]{:S(2)}, u32[]{:S(2)}) async-start(bf16[128,8,768]{2,1,0:T(8,128)(2,1)} %fusion.15), calls=%async_computation.1 | async-start | bytes 3145728 | tf_op jit(solution)/shard_map/all_to_all | solution.py:73
  394.7 76.6 %all-to-all-done.1 = bf16[128,8,768]{2,1,0:T(8,128)(2,1)S(1)} async-done(((bf16[128,8,768]{2,1,0:T(8,128)(2,1)}), bf16[128,8,768]{2,1,0:T(8,128)(2,1)S(1)}, u32[]{:S(2)}, u32[]{:S(2)}) %all-to-all-start.1) | async-done | bytes 1572896 | tf_op jit(solution)/shard_map/all_to_all | solution.py:73
  471.3 3.4 gather_fusion
  (532 shorter events, 217.7 us)
Async XLA Ops:
  6.5 2.7 copy-start
  32.2 21.2 %copy-start.1 = (bf16[1,2,192,2048]{3,2,1,0:T(8,128)(2,1)S(1)}, bf16[1,2,192,2048]{3,2,1,0:T(8,128)(2,1)}, u32[]{:S(2)}) copy-start(bf16[1,2,192,2048]{3,2,1,0:T(8,128)(2,1)} %param.9) | copy-start | bytes 4718596
  32.3 21.4 %copy-start.3 = (s32[1,2,192,128]{3,2,1,0:T(8,128)S(1)}, s32[1,2,192,128]{3,2,1,0:T(8,128)}, u32[]{:S(2)}) copy-start(s32[1,2,192,128]{3,2,1,0:T(8,128)} %param.10) | copy-start | bytes 589828
  32.3 21.7 %slice-start = ((f32[1,128,2048]{2,1,0:T(8,128)}), f32[1,128,128]{2,1,0:T(8,128)S(1)}, s32[]{:S(2)}) async-start(f32[1,128,2048]{2,1,0:T(8,128)} %param.11), calls=%async_computation.3 | async-start | bytes 131072 | tf_op jit(solution)/shard_map/slice | solution.py:21
  32.3 332.2 %all-to-all-start = ((bf16[128,8,2048]{2,1,0:T(8,128)(2,1)}), bf16[128,8,2048]{2,1,0:T(8,128)(2,1)}, u32[]{:S(2)}, u32[]{:S(2)}) async-start(bf16[128,8,2048]{2,1,0:T(8,128)(2,1)} %bitcast.48), calls=%async_computation | async-start | bytes 8388608 | tf_op jit(solution)/shard_map/all_to_all | solution.py:63
  53.4 311.0 %all-gather.2.cloned.1.call-start = ((), (), s32[]{:S(2)}) async-start(), calls=%async_computation.2 | async-start | bytes 7864320 | tf_op jit(solution)/shard_map/all_gather | solution.py:9
  282.4 2.2 copy-start.2
  364.4 6.4 %copy-start.4 = (bf16[768,4096]{1,0:T(8,128)(2,1)S(1)}, bf16[768,4096]{1,0:T(8,128)(2,1)}, u32[]{:S(2)}) copy-start(bf16[768,4096]{1,0:T(8,128)(2,1)} %all-gather.2.cloned.1.call-done) | copy-start | bytes 18874372
  377.9 93.5 %all-to-all-start.1 = ((bf16[128,8,768]{2,1,0:T(8,128)(2,1)}), bf16[128,8,768]{2,1,0:T(8,128)(2,1)S(1)}, u32[]{:S(2)}, u32[]{:S(2)}) async-start(bf16[128,8,768]{2,1,0:T(8,128)(2,1)} %fusion.15), calls=%async_computation.1 | async-start | bytes 3145728 | tf_op jit(solution)/shard_map/all_to_all | solution.py:73
Sparse Core Ops, SparseCore 0:
  290.3 74.0 all-gather.1
where the time goes:
time: 484 us; the launch traced here: 482 us
  other arithmetic  157 us (32%)
  waiting for transfers between devices  151 us (31%)
  local copies, waits for them, and re-layouts  103 us (21%)
  starting transfers between devices  38 us (8%)
  matrix products  17.6 us (4%)
  between operations  13.6 us (3%)
    sub x128, other arithmetic, column(): leading = leading - error_col[..., None] * factor_row[:, None, None, :]  78.2 us
    all_to_all x1, waiting for transfers between devices, local(): lax.all_to_all(hidden_rows, 'expert', split_axis=0, concat_axis=0, tiled=...  76.6 us
    dynamic_slice x128, local copies, waits for them, and re-layouts, column(): lax.dynamic_index_in_dim(factor_row, column_id, 1, keepdims=False)  74.4 us
    all_gather x1, waiting for transfers between devices, in_one_piece(): filled, at, outs = (lax.all_gather(both, axis, axis=dim, tiled=True), 0, [])  74.2 us
    dynamic_update_slice x128, other arithmetic, column(): errors = lax.dynamic_update_index_in_dim(errors, error_col, column_id, 3)  73.4 us
    scatter x1, local copies, waits for them, and re-layouts, local(): jnp.zeros((owners * capacity, model_width), jnp.bfloat16).at[target]  23 us
    all_to_all x1, starting transfers between devices, local(): lax.all_to_all(outbox, 'expert', split_axis=0, concat_axis=0, tiled=True)  21.1 us
    all_to_all x1, starting transfers between devices, local(): lax.all_to_all(hidden_rows, 'expert', split_axis=0, concat_axis=0, tiled=...  16.8 us
  transfers between devices with their start and end apart: 3, of which 2 were waited for; matrix products, arithmetic and copies ran while one was open for 49% of the time, Pallas kernels for 0%

commit v1 on v0

v1 whole, which is shorter than its diff:
```python
import functools

import jax
import jax.numpy as jnp
from jax import lax
from jax.experimental import pallas as pl
from jax.experimental.pallas import tpu as pltpu
from jax.sharding import PartitionSpec as P

MESH = pl.DeviceIdType.MESH
F32 = jnp.float32
BF16 = jnp.bfloat16
HI = lax.Precision.HIGHEST
BLK = 128
SUB = 16
SLOTS = 8
TILE = 256
NY, NZ, NC = 4, 16, 2


def iota(shape, dim):
    return lax.broadcasted_iota(jnp.int32, shape, dim)


def dot(a, b, dims, precision=None):
    return lax.dot_general(
        a, b, (dims, ((), ())), precision=precision, preferred_element_type=F32
    )

def prune_body(w_ref, mask_ref, f_ref, out_ref):
    factor = f_ref[:, :BLK]
    row_id = lax.broadcasted_iota(jnp.int32, (BLK, BLK), 0)
    col_id = lax.broadcasted_iota(jnp.int32, (BLK, BLK), 1)
    diagonal = jnp.sum(jnp.where(row_id == col_id, factor, 0.0), axis=1, keepdims=True)
    factor_t = factor.T
    lead = w_ref[:, :BLK].astype(F32).T
    scale = (1 - mask_ref[...]).astype(F32).T / diagonal
    errors, done = [], []
    for start in range(0, BLK, SUB):
        part = lead[:SUB]
        rows = []
        for i in range(SUB):
            g = start + i
            err = part[i : i + 1] * scale[g : g + 1]
            part = part - factor_t[start : start + SUB, g : g + 1] * err
            rows.append(err)
        block = jnp.concatenate(rows, axis=0)
        errors.append(block)
        done.append(part)
        if start + SUB < BLK:
            upd = lax.dot_general(
                factor[start : start + SUB], block, (((0,), (0,)), ((), ())),
                precision=HI, preferred_element_type=F32,
            )
            lead = lead[SUB:] - upd[start + SUB :]
    err_all = jnp.concatenate(errors, axis=0).T
    out_ref[:, :BLK] = jnp.concatenate(done, axis=0).T.astype(out_ref.dtype)
    step = 384
    for at in range(BLK, w_ref.shape[1], step):
        upd = lax.dot_general(
            err_all, f_ref[:, at : at + step], (((1,), (0,)), ((), ())),
            precision=HI, preferred_element_type=F32,
        )
        out_ref[:, at : at + step] = (w_ref[:, at : at + step].astype(F32) - upd).astype(out_ref.dtype)


def prune(weights, keep_mask, inv_factor):
    p, r, d = weights.shape[1:]
    return pl.pallas_call(
        prune_body,
        out_shape=jax.ShapeDtypeStruct((p * r, d), jnp.bfloat16),
        in_specs=[pl.BlockSpec(memory_space=pltpu.VMEM)] * 3,
        out_specs=pl.BlockSpec(memory_space=pltpu.VMEM),
        name="prune",
    )(weights.reshape(p * r, d), keep_mask.reshape(p * r, BLK), inv_factor.reshape(BLK, d))


def exchange_body(nx, tok, routes, pruned, out, t_up, t_down, rt_own, rt, packed, rows, whole, batch_rows,
                  hid, back, home, code, bar_sems, ring_s, ring_r, rt_s, rt_r, x_s, x_r, own_s,
                  ys_s, ys_r, zs_s, zs_r, hs_s, hs_r, loc_s):
    del bar_sems
    tokens, width = tok.shape
    top = routes.shape[1]
    slots_all = tokens * top
    own_rows = pruned.shape[0] // 2
    half = NZ // 2
    peers = NY * NC
    batch = min(4, NZ)
    batches = NZ // batch
    x = lax.axis_index("dp")
    me = lax.axis_index("expert")
    y = me // (NZ * NC)
    z = (me // NC) % NZ
    c = me % NC

    def along_z(n):
        return {"expert": (y * NZ + (z + n) % NZ) * NC + c}

    def along_y(q):
        return {"expert": (((y + q // NC) % NY) * NZ + z) * NC + (c + q % NC) % NC}

    def along_x(n):
        return {"dp": (x + n) % nx}

    def mirror(q):
        return ((NY - q // NC) % NY) * NC + q % NC

    def remote(src, dst, s, r, device):
        return pltpu.make_async_remote_copy(
            src_ref=src, dst_ref=dst, send_sem=s, recv_sem=r, device_id=device, device_id_type=MESH
        )

    barrier = pltpu.get_barrier_semaphore()
    met = [along_z(n) for n in range(1, NZ)] + [along_y(q) for q in range(1, peers)]
    if nx > 1:
        met += [along_x(1), along_x(nx - 1)]
    for device in met:
        pl.semaphore_signal(barrier, inc=1, device_id=device, device_id_type=MESH)
    pl.semaphore_wait(barrier, len(met))

    part = tokens // 2

    def ring(way, s, h):
        span = pl.ds(h * part, part)
        held = t_up if way == 0 or s == half else t_down
        before = t_up if way == 0 else t_down
        src = tok.at[span] if s == 1 else before.at[s - 1, span]
        at = (s * 2 + way) * 2 + h
        return remote(src, held.at[s, span], ring_s.at[at], ring_r.at[at], along_z(1 if way == 0 else NZ - 1))

    def ring_has(way, s, h):
        return s < half or (s == half and h == way)

    for h in range(2):
        for way in range(2):
            if ring_has(way, 1, h):
                ring(way, 1, h).start()

    x_copies, x_forward = [], []
    span_own = [pl.ds(g * own_rows, own_rows) for g in range(2)]

    def place(g, n):
        return whole.at[g, pl.ds(pl.multiple_of(((x + n) % nx) * own_rows, own_rows), own_rows)]

    own_copies = [pltpu.make_async_copy(pruned.at[span_own[g]], place(g, 0), own_s.at[g]) for g in range(2)]
    for copy in own_copies:
        copy.start()
    if nx > 1:
        for i, (n, g) in enumerate(((1, 0), (nx - 1, 1), (1, 1), (nx - 1, 0))):
            copy = remote(pruned.at[span_own[g]], place(g, 0), x_s.at[i], x_r.at[i], along_x(n))
            copy.start()
            x_copies.append(copy)

    chosen = routes[...].astype(F32).astype(BF16)
    eye = (iota((tokens, BLK), 0) == iota((tokens, BLK), 1)).astype(F32).astype(BF16)
    turned = dot(chosen, eye, ((0,), (0,)))
    turned = jnp.where(iota((top, BLK), 1) < tokens, turned, -1.0)
    rt_own[...] = turned
    rt[0] = turned

    repeat = (iota((slots_all, tokens), 0) // top == iota((slots_all, tokens), 1)).astype(F32).astype(BF16)
    spread = dot(repeat, chosen, ((1,), (0,)))
    mine = iota((slots_all, top), 0) % top == iota((slots_all, top), 1)
    expert_of = jnp.sum(jnp.where(mine, spread, 0.0), axis=1, keepdims=True)
    hot = (expert_of == iota((slots_all, NY * NZ * NC), 1).astype(F32)).astype(F32)
    earlier = (iota((slots_all, slots_all), 1) < iota((slots_all, slots_all), 0)).astype(F32).astype(BF16)
    ranks = dot(earlier, hot.astype(BF16), ((1,), (0,)))
    each = iota((1, NY * NZ * NC), 1)
    rel = (each // NC % NZ - z + NZ) % NZ
    pos = jnp.where(rel < half, 2 * (half - rel), 2 * (rel - half) + 1)
    pos = jnp.where(rel == half, 0, jnp.where(rel == 0, 1, pos))
    peer = (each // (NZ * NC) - y + NY) % NY * NC + (each % NC - c + NC) % NC
    table = ((pos * peers + peer) * SLOTS).astype(F32)
    code[...] = jnp.broadcast_to(jnp.sum(hot * (ranks + table), axis=1, keepdims=True), code.shape)

    if NZ > 1:
        for n in range(1, NZ):
            remote(rt_own, rt.at[(NZ - n) % NZ], rt_s, rt_r, along_z(n)).start()
        pltpu.make_async_copy(rt.at[pl.ds(1, NZ - 1)], rt.at[pl.ds(1, NZ - 1)], rt_r).wait()

    q_id = iota((peers, BLK), 0)
    experts = (((y + q_id // NC) % NY * NZ + z) * NC + (c + q_id % NC) % NC).astype(F32)
    before_token = (iota((BLK, BLK), 0) < iota((BLK, BLK), 1)).astype(F32).astype(BF16)

    def pack(position, n, block):
        named = rt[n]
        hit = jnp.zeros((peers, BLK), F32)
        for k in range(top):
            hit = hit + (named[k : k + 1] == experts).astype(F32)
        rank = dot(hit.astype(BF16), before_token, ((1,), (0,)))
        key = jnp.where(hit > 0, rank, -1.0)
        pick = (key[:, None, :] == iota((peers, SLOTS, BLK), 1).astype(F32)).astype(F32)
        pick = pick.reshape(peers * SLOTS, BLK).astype(BF16)[:, :tokens]
        for at in range(0, width, min(512, width)):
            cols = pl.ds(at, min(512, width))
            taken = dot(pick, block[:, cols], ((1,), (0,)))
            taken = taken.reshape(peers, SLOTS, min(512, width)).astype(BF16)
            packed[position, :, :, cols] = taken
            rows[position, 0, :, cols] = taken[0]

    def to_peer(position, q):
        return remote(packed.at[position, q], rows.at[position, mirror(q)], ys_s.at[position], ys_r.at[position], along_y(q))

    def hand_out(position):
        for q in range(1, peers):
            to_peer(position, q).start()

    pack(1, 0, tok)
    hand_out(1)
    for s in range(1, half + 1):
        for h in range(2):
            for way in range(2):
                if ring_has(way, s, h):
                    ring(way, s, h).wait_recv()
                    if ring_has(way, s + 1, h):
                        ring(way, s + 1, h).start()
        if nx > 1 and s == min(3, half):
            x_copies[0].wait_recv()
            x_copies[1].wait_recv()
            for i, (g, n) in enumerate(((0, 1), (1, nx - 1))):
                copy = remote(place(g, nx - n), place(g, nx - n), x_s.at[4 + i], x_r.at[4 + i], along_x(n))
                copy.start()
                x_forward.append(copy)
        if s < half:
            pack(2 * (half - s), s, t_down.at[s])
            pack(2 * (half - s) + 1, NZ - s, t_up.at[s])
            hand_out(2 * (half - s))
            hand_out(2 * (half - s) + 1)
        else:
            pack(0, half, t_up.at[half])
            hand_out(0)

    for copy in own_copies:
        copy.wait()
    for copy in x_copies[2:] + x_forward:
        copy.wait_recv()

    def to_line(m, later):
        p = 2 * m + later
        n = half + m if later else half - m
        return remote(hid.at[p], back.at[2 * m + 1 - later], zs_s.at[p], zs_r.at[2 * m + 1 - later], along_z(n))

    far = remote(hid.at[0], back.at[0], zs_s.at[0], zs_r.at[0], along_z(half))
    here = pltpu.make_async_copy(hid.at[1], back.at[1], zs_r.at[1])

    def work(b, carry):
        first = b * batch
        for k in range(batch):
            if peers > 1:
                landed = rows.at[first + k, pl.ds(1, peers - 1)]
                pltpu.make_async_copy(landed, landed, ys_r.at[first + k]).wait()
        count = batch * peers * SLOTS
        batch_rows[...] = rows[pl.ds(first, batch)].astype(F32).reshape(count, width).astype(BF16)
        for at in range(0, whole.shape[1], TILE):
            cols = pl.ds(at, TILE)
            gate = dot(batch_rows[...], whole[0, cols], ((1,), (1,)))
            up = dot(batch_rows[...], whole[1, cols], ((1,), (1,)))
            value = gate / (1.0 + jnp.exp(-gate)) * up
            hid[pl.ds(first, batch), :, :, cols] = value.reshape(batch, peers, SLOTS, TILE).astype(BF16)

        @pl.when(b == 0)
        def _():
            far.start()
            here.start()

        @pl.when(b > 0)
        def _():
            to_line(b * (batch // 2), 0).start()
            to_line(b * (batch // 2), 1).start()

        for j in range(1, batch // 2):
            to_line(b * (batch // 2) + j, 0).start()
            to_line(b * (batch // 2) + j, 1).start()
        return carry

    lax.fori_loop(0, batches, work, 0)

    def homeward(b, q):
        span = pl.ds(b * batch, batch)
        return remote(back.at[span, q], home.at[span, mirror(q)], hs_s.at[b], hs_r.at[b], along_y(q))

    def stay(b):
        span = pl.ds(b * batch, batch)
        return pltpu.make_async_copy(back.at[span, 0], home.at[span, 0], loc_s.at[b])

    out[...] = jnp.zeros(out.shape, out.dtype)

    def finish(b, carry):
        @pl.when(b < batches)
        def _():
            for k in range(batch):
                block = back.at[b * batch + k]
                pltpu.make_async_copy(block, block, zs_r.at[b * batch + k]).wait()
            stay(b).start()
            for q in range(1, peers):
                homeward(b, q).start()

        @pl.when(b > 0)
        def _():
            last = b - 1
            span = pl.ds(last * batch, batch)
            stay(last).wait()
            if peers > 1:
                landed = home.at[span, pl.ds(1, peers - 1)]
                pltpu.make_async_copy(landed, landed, hs_r.at[last]).wait()
            count = batch * peers * SLOTS
            values = home[span].astype(F32).reshape(count, out.shape[1]).astype(BF16)
            wanted = (iota((slots_all, BLK), 1) + last * count).astype(F32)
            pick = [(code[...] == wanted + float(at)).astype(F32).astype(BF16) for at in range(0, count, BLK)]
            pick = jnp.concatenate(pick, axis=1)[:, :count]
            for at in range(0, out.shape[1], TILE):
                cols = pl.ds(at, TILE)
                got = dot(pick, values[:, at : at + TILE], ((1,), (0,)))
                out[:, cols] = (out[:, cols].astype(F32) + got).astype(BF16)
        return carry

    lax.fori_loop(0, batches + 1, finish, 0)

    for s in range(1, half + 1):
        for h in range(2):
            for way in range(2):
                if ring_has(way, s, h):
                    ring(way, s, h).wait_send()
    for copy in x_copies + x_forward:
        copy.wait_send()
    if NZ > 1:
        pltpu.make_async_copy(rt.at[pl.ds(1, NZ - 1)], rt.at[pl.ds(1, NZ - 1)], rt_s).wait()

    def drain(p, carry):
        if peers > 1:
            pltpu.make_async_copy(packed.at[p, pl.ds(1, peers - 1)], packed.at[p, pl.ds(1, peers - 1)], ys_s.at[p]).wait()

        @pl.when(p != 1)
        def _():
            pltpu.make_async_copy(hid.at[p], hid.at[p], zs_s.at[p]).wait()
        return carry

    lax.fori_loop(0, NZ, drain, 0)

    def drain_home(b, carry):
        if peers > 1:
            sent = back.at[pl.ds(b * batch, batch), pl.ds(1, peers - 1)]
            pltpu.make_async_copy(sent, sent, hs_s.at[b]).wait()
        return carry

    lax.fori_loop(0, batches, drain_home, 0)


def exchange(tokens, routes, pruned):
    nx = lax.axis_size("dp")
    count, width = tokens.shape
    top = routes.shape[1]
    hidden = pruned.shape[0] // 2 * nx
    half, peers = NZ // 2, NY * NC
    batch = min(4, NZ)
    dma = pltpu.SemaphoreType.DMA
    out = pl.pallas_call(
        functools.partial(exchange_body, nx),
        out_shape=jax.ShapeDtypeStruct((count * top, hidden), BF16),
        in_specs=[pl.BlockSpec(memory_space=pltpu.VMEM)] * 3,
        out_specs=pl.BlockSpec(memory_space=pltpu.VMEM),
        scratch_shapes=[
            pltpu.VMEM((half + 1, count, width), BF16),
            pltpu.VMEM((half, count, width), BF16),
            pltpu.VMEM((top, BLK), F32),
            pltpu.VMEM((NZ, top, BLK), F32),
            pltpu.VMEM((NZ, peers, SLOTS, width), BF16),
            pltpu.VMEM((NZ, peers, SLOTS, width), BF16),
            pltpu.VMEM((2, hidden, width), BF16),
            pltpu.VMEM((batch * peers * SLOTS, width), BF16),
            pltpu.VMEM((NZ, peers, SLOTS, hidden), BF16),
            pltpu.VMEM((NZ, peers, SLOTS, hidden), BF16),
            pltpu.VMEM((NZ, peers, SLOTS, hidden), BF16),
            pltpu.VMEM((count * top, BLK), F32),
            dma((1,)),
            dma(((half + 1) * 4,)),
            dma(((half + 1) * 4,)),
            dma(()),
            dma(()),
            dma((6,)),
            dma((6,)),
            dma((2,)),
            dma((NZ,)),
            dma((NZ,)),
            dma((NZ,)),
            dma((NZ,)),
            dma((NZ // batch,)),
            dma((NZ // batch,)),
            dma((NZ // batch,)),
        ],
        compiler_params=pltpu.CompilerParams(
            collective_id=0, has_side_effects=True, vmem_limit_bytes=60 * 1024 * 1024
        ),
        name="exchange",
    )(tokens, routes, pruned)
    return out.reshape(count, top, hidden)


def local(tokens, routes, weights, keep_mask, inv_factor):
    pruned = prune(weights, keep_mask, inv_factor)
    return exchange(tokens, routes, pruned)


def solution(mesh):
    return jax.shard_map(
        local,
        mesh=mesh,
        in_specs=(
            P(("dp", "expert"), None),
            P(("dp", "expert"), None),
            P("expert", None, "dp", None),
            P("expert", None, "dp", None),
            P("expert", None, None),
        ),
        out_specs=P(("dp", "expert"), None, None),
        check_vma=False,
    )
```

time: 484 us -> 191 us (0.39)
  Pallas kernels: 0 us -> 187 us
  other arithmetic: 157 us -> 0 us
  waiting for transfers between devices: 151 us -> 0 us
  local copies, waits for them, and re-layouts: 103 us -> 3.76 us
  starting transfers between devices: 38 us -> 0 us
  matrix products: 17.6 us -> 0 us
  between operations: 13.6 us -> 0.01 us
    pallas_call x0 -> x2, Pallas kernels: none -> 187 us  [the longest x1 178 us: exchange(): pl.pallas_call(functools.partial(exchange_body, nx), out_shape=jax.ShapeD...]
    sub x129 -> x0, other arithmetic: 78.2 us -> none  [the longest x128 78.2 us: column(): leading = leading - error_col[..., None] * factor_row[:, None, None, :]]
    all_to_all x2 -> x0, waiting for transfers between devices: 76.6 us -> none  [the longest x1 76.6 us: local(): lax.all_to_all(hidden_rows, 'expert', split_axis=0, concat_axis=0, tiled=...]
    dynamic_slice x128 -> x0, local copies, waits for them, and re-layouts: 74.4 us -> none  [column(): lax.dynamic_index_in_dim(factor_row, column_id, 1, keepdims=False)]
    all_gather x1 -> x0, waiting for transfers between devices: 74.2 us -> none  [in_one_piece(): filled, at, outs = (lax.all_gather(both, axis, axis=dim, tiled=True), 0, [])]
    dynamic_update_slice x128 -> x0, other arithmetic: 73.4 us -> none  [column(): errors = lax.dynamic_update_index_in_dim(errors, error_col, column_id, 3)]
    all_to_all x2 -> x0, starting transfers between devices: 37.9 us -> none  [the longest x1 21.1 us: local(): lax.all_to_all(outbox, 'expert', split_axis=0, concat_axis=0, tiled=True)]
    scatter x1 -> x0, local copies, waits for them, and re-layouts: 23 us -> none  [local(): jnp.zeros((owners * capacity, model_width), jnp.bfloat16).at[target]]
  transfers between devices with their start and end apart: 3 -> 0, of which waited for: 2 -> 0; matrix products, arithmetic and copies ran while one was open for 49% -> 0% of each run, Pallas kernels for 0% -> 0%
where the time goes in v1:
time: 191 us; the launch traced here: 190 us
  Pallas kernels  187 us (98%)
  local copies, waits for them, and re-layouts  3.76 us (2%)
    pallas_call x1, Pallas kernels, exchange(): pl.pallas_call(functools.partial(exchange_body, nx), out_shape=jax.ShapeD...  178 us
    pallas_call x1, Pallas kernels, prune(): pl.pallas_call(prune_body, out_shape=jax.ShapeDtypeStruct((p * r, d), jnp...  8.59 us

profile of v1, /device:TPU:1, one launch (start us, length us, event | category | flops | bytes accessed | tf_op | source)
XLA Modules:
  0.0 190.3 jit_solution(1741748305064462490)
XLA Ops:
  0.0 1.4 copy.6.routes
  1.4 8.6 %prune.1.pruned = bf16[384,2048]{1,0:T(8,128)(2,1)} custom-call(bf16[384,2048]{1,0:T(8,128)(2,1)} %bitcast.5, s32[384,128]{1,0:T(8,128)} %bitcast.7, f32[128,2048]{1,0:T(8,128)} %bitcast.6), custom_call_target="tpu_custom_call" | custom-call | tf_op jit(solution)/shard_map/prune/pallas_call | solution.py:69
  10.0 178.0 %exchange.1 = bf16[768,768]{1,0:T(8,128)(2,1)} custom-call(bf16[96,2048]{1,0:T(8,128)(2,1)} %tok.1, s32[96,8]{1,0:T(8,128)} %copy.6.routes, bf16[384,2048]{1,0:T(8,128)(2,1)} %prune.1.pruned), custom_call_target="tpu_custom_call" | custom-call | tf_op jit(solution)/shard_map/exchange/pallas_call | solution.py:357
  188.0 2.4 %copy.8 = bf16[96,8,768]{2,1,0:T(8,128)(2,1)} copy(bf16[96,8,768]{2,1,0:T(8,128)(2,1)} %bitcast.4) | data formatting | bytes 2359296

commit v2 on v1

v2 whole, which is shorter than its diff:
```python
import functools

import jax
import jax.numpy as jnp
from jax import lax
from jax.experimental import pallas as pl
from jax.experimental.pallas import tpu as pltpu
from jax.sharding import PartitionSpec as P

MESH = pl.DeviceIdType.MESH
F32 = jnp.float32
BF16 = jnp.bfloat16
HI = lax.Precision.HIGHEST
BLK = 128
SUB = 16
SLOTS = 8
TILE = 256
CHUNKS = 3
X_STEP = 3
VMEM_MIB = 60
FAR_MET = ()
NY, NZ, NC = 4, 16, 2
ORDER = (4, 5, 3, 6, 7, 8, 1, 2)
EARLY = {7: (0,)}


def iota(shape, dim):
    return lax.broadcasted_iota(jnp.int32, shape, dim)


def dot(a, b, dims, precision=None):
    return lax.dot_general(
        a, b, (dims, ((), ())), precision=precision, preferred_element_type=F32
    )


def prune_body(w_ref, mask_ref, f_ref, out_ref):
    factor = f_ref[:, :BLK]
    row_id = lax.broadcasted_iota(jnp.int32, (BLK, BLK), 0)
    col_id = lax.broadcasted_iota(jnp.int32, (BLK, BLK), 1)
    diagonal = jnp.sum(jnp.where(row_id == col_id, factor, 0.0), axis=1, keepdims=True)
    factor_t = factor.T
    lead = w_ref[:, :BLK].astype(F32).T
    scale = (1 - mask_ref[...]).astype(F32).T / diagonal
    errors, done = [], []
    for start in range(0, BLK, SUB):
        part = lead[:SUB]
        rows = []
        for i in range(SUB):
            g = start + i
            err = part[i : i + 1] * scale[g : g + 1]
            part = part - factor_t[start : start + SUB, g : g + 1] * err
            rows.append(err)
        block = jnp.concatenate(rows, axis=0)
        errors.append(block)
        done.append(part)
        if start + SUB < BLK:
            upd = lax.dot_general(
                factor[start : start + SUB], block, (((0,), (0,)), ((), ())),
                precision=HI, preferred_element_type=F32,
            )
            lead = lead[SUB:] - upd[start + SUB :]
    err_all = jnp.concatenate(errors, axis=0).T
    out_ref[:, :BLK] = jnp.concatenate(done, axis=0).T.astype(out_ref.dtype)
    step = 384
    for at in range(BLK, w_ref.shape[1], step):
        upd = lax.dot_general(
            err_all, f_ref[:, at : at + step], (((1,), (0,)), ((), ())),
            precision=HI, preferred_element_type=F32,
        )
        out_ref[:, at : at + step] = (w_ref[:, at : at + step].astype(F32) - upd).astype(out_ref.dtype)


def exchange_body(nx, tok_in, routes_in, weights_in, mask_in, factor_in, out, tok, weights, mask, factor, pruned,
                  t_up, t_down, rt, packed, rows, whole, batch_rows, hid, back, home, code, load_s, ring_s, ring_r,
                  rt_s, rt_r, x_s, x_r, own_s, ys_s, ys_r, zs_s, zs_r, hs_s, hs_r, loc_s):
    tokens, width = tok.shape
    top = routes_in.shape[0]
    slots_all = tokens * top
    own_rows = pruned.shape[0] // 2
    half = NZ // 2
    peers = NY * NC
    owners = NY * NZ * NC
    order = [n for s in ORDER for n in ((s, NZ - s) if s < half else (half, 0))]
    pos_of = {n: p for p, n in enumerate(order)}
    batch = min(4, NZ)
    batches = NZ // batch
    x = lax.axis_index("dp")
    me = lax.axis_index("expert")
    y = me // (NZ * NC)
    z = (me // NC) % NZ
    c = me % NC

    loads = [
        pltpu.make_async_copy(src, dst, load_s.at[i])
        for i, (src, dst) in enumerate(((tok_in, tok), (weights_in, weights), (mask_in, mask), (factor_in, factor)))
    ]
    for copy in loads:
        copy.start()

    def along_z(n):
        return {"expert": (y * NZ + (z + n) % NZ) * NC + c}

    def along_y(q):
        return {"expert": (((y + q // NC) % NY) * NZ + z) * NC + (c + q % NC) % NC}

    def along_x(n):
        return {"dp": (x + n) % nx}

    def mirror(q):
        return ((NY - q // NC) % NY) * NC + q % NC

    def remote(src, dst, s, r, device):
        return pltpu.make_async_remote_copy(
            src_ref=src, dst_ref=dst, send_sem=s, recv_sem=r, device_id=device, device_id_type=MESH
        )

    barrier = pltpu.get_barrier_semaphore()
    met = [along_z(n) for n in (FAR_MET if FAR_MET else sorted({1, NZ - 1}))] + [along_y(q) for q in range(1, peers)]
    if nx > 1:
        met += [along_x(1), along_x(nx - 1)]
    for device in met:
        pl.semaphore_signal(barrier, inc=1, device_id=device, device_id_type=MESH)
    pl.semaphore_wait(barrier, len(met))

    chunk = tokens // CHUNKS

    def ring_rows(way, s, h):
        low, high = h * chunk, h * chunk + chunk
        if s == half:
            low, high = (low, min(high, tokens // 2)) if way == 0 else (max(low, tokens // 2), high)
        return low, high

    def ring_has(way, s, h):
        low, high = ring_rows(way, s, h)
        return s <= half and low < high

    def ring(way, s, h):
        low, high = ring_rows(way, s, h)
        span = pl.ds(low, high - low)
        held = t_up if way == 0 or s == half else t_down
        src = tok.at[span] if s == 1 else (t_up if way == 0 else t_down).at[s - 1, span]
        at = ((s - 1) * 2 + way) * CHUNKS + h
        return remote(src, held.at[s, span], ring_s.at[at], ring_r.at[at], along_z(1 if way == 0 else NZ - 1))

    def names(way, s):
        at = (s - 1) * 2 + way
        src, dst = (NZ - s + 1) % NZ if way == 0 else s - 1, NZ - s if way == 0 else s
        return remote(rt.at[src], rt.at[dst], rt_s.at[at], rt_r.at[at], along_z(1 if way == 0 else NZ - 1))

    def names_has(way, s):
        return s < half or (s == half and way == 0)

    loads[0].wait()
    for h in range(CHUNKS):
        for way in range(2):
            if ring_has(way, 1, h):
                ring(way, 1, h).start()

    rt[0] = jnp.full((top, BLK), -1.0, F32)
    rt[0, :, pl.ds(0, tokens)] = routes_in[...].astype(F32)

    for copy in loads[1:]:
        copy.wait()
    prune_body(weights, mask, factor, pruned)

    x_copies, x_forward = [], []
    span_own = [pl.ds(g * own_rows, own_rows) for g in range(2)]

    def place(g, n):
        return whole.at[g, pl.ds(pl.multiple_of(((x + n) % nx) * own_rows, own_rows), own_rows)]

    for way in range(2):
        if names_has(way, 1):
            names(way, 1).start()
    own_copies = [pltpu.make_async_copy(pruned.at[span_own[g]], place(g, 0), own_s.at[g]) for g in range(2)]
    if nx > 1:
        for i, (n, g) in enumerate(((1, 0), (nx - 1, 1), (1, 1), (nx - 1, 0))):
            copy = remote(pruned.at[span_own[g]], place(g, 0), x_s.at[i], x_r.at[i], along_x(n))
            copy.start()
            x_copies.append(copy)
    for copy in own_copies:
        copy.start()

    def forward_weights():
        if nx > 1:
            x_copies[0].wait_recv()
            x_copies[1].wait_recv()
            for i, (g, n) in enumerate(((0, 1), (1, nx - 1))):
                copy = remote(place(g, nx - n), place(g, nx - n), x_s.at[4 + i], x_r.at[4 + i], along_x(n))
                copy.start()
                x_forward.append(copy)

    def find_code():
        lane = (iota((tokens, BLK), 0) == iota((tokens, BLK), 1)).astype(F32).astype(BF16)
        chosen = dot(lane, rt[0].astype(BF16), ((1,), (1,))).astype(BF16)
        repeat = (iota((slots_all, tokens), 0) // top == iota((slots_all, tokens), 1)).astype(F32).astype(BF16)
        spread = dot(repeat, chosen, ((1,), (0,)))
        mine = iota((slots_all, top), 0) % top == iota((slots_all, top), 1)
        expert_of = jnp.sum(jnp.where(mine, spread, 0.0), axis=1, keepdims=True)
        hot = (expert_of == iota((slots_all, owners), 1).astype(F32)).astype(F32)
        earlier = (iota((slots_all, slots_all), 1) < iota((slots_all, slots_all), 0)).astype(F32).astype(BF16)
        ranks = dot(earlier, hot.astype(BF16), ((1,), (0,)))
        each = iota((1, owners), 1)
        rel = (each // NC % NZ - z + NZ) % NZ
        pos = jnp.zeros_like(rel)
        for n, p in pos_of.items():
            pos = jnp.where(rel == n, p, pos)
        peer = (each // (NZ * NC) - y + NY) % NY * NC + (each % NC - c + NC) % NC
        table = ((pos * peers + peer) * SLOTS).astype(F32)
        code[...] = jnp.broadcast_to(jnp.sum(hot * (ranks + table), axis=1, keepdims=True), code.shape)

    q_id = iota((peers, BLK), 0)
    experts = (((y + q_id // NC) % NY * NZ + z) * NC + (c + q_id % NC) % NC).astype(F32)
    before_token = (iota((BLK, BLK), 0) < iota((BLK, BLK), 1)).astype(F32).astype(BF16)

    def pack(n, block):
        position = pos_of[n]
        named = rt[n]
        hit = jnp.zeros((peers, BLK), F32)
        for k in range(top):
            hit = hit + (named[k : k + 1] == experts).astype(F32)
        rank = dot(hit.astype(BF16), before_token, ((1,), (0,)))
        key = jnp.where(hit > 0, rank, -1.0)
        pick = (key[:, None, :] == iota((peers, SLOTS, BLK), 1).astype(F32)).astype(F32)
        pick = pick.reshape(peers * SLOTS, BLK).astype(BF16)[:, :tokens]
        wide = min(512, width)
        for at in range(0, width, wide):
            cols = pl.ds(at, wide)
            taken = dot(pick, block[:, cols], ((1,), (0,)))
            taken = taken.reshape(peers, SLOTS, wide).astype(BF16)
            packed[position, :, :, cols] = taken
            rows[position, 0, :, cols] = taken[0]

    def to_peer(position, q):
        return remote(packed.at[position, q], rows.at[position, mirror(q)], ys_s.at[position], ys_r.at[position], along_y(q))

    packed_last = []

    def pack_next(n, block):
        pack(n, block)
        hand_out()
        packed_last.append(pos_of[n])

    def hand_out():
        while packed_last:
            position = packed_last.pop()
            for q in range(1, peers):
                to_peer(position, q).start()

    def return_to(n):
        p, q = pos_of[n], pos_of[(NZ - n) % NZ]
        if n == 0:
            return pltpu.make_async_copy(hid.at[p], back.at[p], zs_r.at[p])
        return remote(hid.at[p], back.at[q], zs_s.at[p], zs_r.at[q], along_z(n))

    def work(b):
        first = b * batch
        if peers > 1:
            for k in range(batch):
                landed = rows.at[first + k, pl.ds(1, peers - 1)]
                pltpu.make_async_copy(landed, landed, ys_r.at[first + k]).wait()
        count = batch * peers * SLOTS
        batch_rows[...] = rows[pl.ds(first, batch)].astype(F32).reshape(count, width).astype(BF16)
        for at in range(0, whole.shape[1], TILE):
            cols = pl.ds(at, TILE)
            gate = dot(batch_rows[...], whole[0, cols], ((1,), (1,)))
            up = dot(batch_rows[...], whole[1, cols], ((1,), (1,)))
            value = gate / (1.0 + jnp.exp(-gate)) * up
            hid[pl.ds(first, batch), :, :, cols] = value.reshape(batch, peers, SLOTS, TILE).astype(BF16)
        for n in sorted(order[first : first + batch], key=lambda n: -min(n, NZ - n)):
            return_to(n).start()

    def have_weights():
        for copy in own_copies:
            copy.wait()
        for copy in x_copies[2:] + x_forward:
            copy.wait_recv()

    jobs = {(1, 0): [lambda: pack_next(0, tok)], (1, 1): [find_code]}
    for s in range(1, half):
        jobs.setdefault((s + 1, 0), []).append(lambda s=s: pack_next(NZ - s, t_up.at[s]))
        jobs.setdefault((s + 1, 1), []).append(lambda s=s: pack_next(s, t_down.at[s]))
    jobs.setdefault((min(X_STEP, half), 2), []).append(forward_weights)
    for s, early in EARLY.items():
        jobs.setdefault((s, CHUNKS - 1), []).append(have_weights)
        for b in early:
            jobs[s, CHUNKS - 1].append(lambda b=b: work(b))
    for s in range(1, half + 1):
        for h in range(CHUNKS):
            for way in range(2):
                if h == 0 and names_has(way, s):
                    names(way, s).wait_recv()
                    if names_has(way, s + 1):
                        names(way, s + 1).start()
                if ring_has(way, s, h):
                    ring(way, s, h).wait_recv()
                    if ring_has(way, s + 1, h):
                        ring(way, s + 1, h).start()
            for job in jobs.get((s, h), []):
                job()
    pack_next(half, t_up.at[half])
    hand_out()
    if not EARLY:
        have_weights()
    for b in range(batches):
        if not any(b in early for early in EARLY.values()):
            work(b)

    def homeward(b, q):
        span = pl.ds(b * batch, batch)
        return remote(back.at[span, q], home.at[span, mirror(q)], hs_s.at[b], hs_r.at[b], along_y(q))

    def stay(b):
        span = pl.ds(b * batch, batch)
        return pltpu.make_async_copy(back.at[span, 0], home.at[span, 0], loc_s.at[b])

    def send_home(b):
        for k in range(batch):
            block = back.at[b * batch + k]
            pltpu.make_async_copy(block, block, zs_r.at[b * batch + k]).wait()
        stay(b).start()
        for q in range(1, peers):
            homeward(b, q).start()

    def unpack(b):
        span = pl.ds(b * batch, batch)
        stay(b).wait()
        if peers > 1:
            landed = home.at[span, pl.ds(1, peers - 1)]
            pltpu.make_async_copy(landed, landed, hs_r.at[b]).wait()
        count = batch * peers * SLOTS
        values = home[span].astype(F32).reshape(count, out.shape[1]).astype(BF16)
        lanes = iota((slots_all, BLK), 1).astype(F32)
        pick = [(code[...] == lanes + float(b * count + at)).astype(F32).astype(BF16) for at in range(0, count, BLK)]
        pick = jnp.concatenate(pick, axis=1)[:, :count]
        for at in range(0, out.shape[1], TILE):
            cols = pl.ds(at, TILE)
            got = dot(pick, values[:, at : at + TILE], ((1,), (0,)))
            if b > 0:
                got = out[:, cols].astype(F32) + got
            out[:, cols] = got.astype(BF16)

    for b in range(batches):
        send_home(b)
        if b > 0:
            unpack(b - 1)
    unpack(batches - 1)

    for s in range(1, half + 1):
        for way in range(2):
            if names_has(way, s):
                names(way, s).wait_send()
            for h in range(CHUNKS):
                if ring_has(way, s, h):
                    ring(way, s, h).wait_send()
    for copy in x_copies + x_forward:
        copy.wait_send()
    for p in range(NZ):
        if peers > 1:
            sent = packed.at[p, pl.ds(1, peers - 1)]
            pltpu.make_async_copy(sent, sent, ys_s.at[p]).wait()
        if order[p] != 0:
            pltpu.make_async_copy(hid.at[p], hid.at[p], zs_s.at[p]).wait()
    if peers > 1:
        for b in range(batches):
            sent = back.at[pl.ds(b * batch, batch), pl.ds(1, peers - 1)]
            pltpu.make_async_copy(sent, sent, hs_s.at[b]).wait()


def exchange(tokens, routes, weights, keep_mask, factor):
    nx = lax.axis_size("dp")
    count, width = tokens.shape
    top = routes.shape[1]
    own = weights.shape[0]
    hidden = own // 2 * nx
    half, peers = NZ // 2, NY * NC
    batch = min(4, NZ)
    dma = pltpu.SemaphoreType.DMA
    vmem = pltpu.VMEM
    out = pl.pallas_call(
        functools.partial(exchange_body, nx),
        out_shape=jax.ShapeDtypeStruct((count * top, hidden), BF16),
        in_specs=[
            pl.BlockSpec(memory_space=pltpu.HBM),
            pl.BlockSpec(memory_space=pltpu.VMEM),
            pl.BlockSpec(memory_space=pltpu.HBM),
            pl.BlockSpec(memory_space=pltpu.HBM),
            pl.BlockSpec(memory_space=pltpu.HBM),
        ],
        out_specs=pl.BlockSpec(memory_space=pltpu.VMEM),
        scratch_shapes=[
            vmem((count, width), BF16),
            vmem((own, width), BF16),
            vmem((own, BLK), jnp.int32),
            vmem((BLK, width), F32),
            vmem((own, width), BF16),
            vmem((half + 1, count, width), BF16),
            vmem((half, count, width), BF16),
            vmem((NZ, top, BLK), F32),
            vmem((NZ, peers, SLOTS, width), BF16),
            vmem((NZ, peers, SLOTS, width), BF16),
            vmem((2, hidden, width), BF16),
            vmem((batch * peers * SLOTS, width), BF16),
            vmem((NZ, peers, SLOTS, hidden), BF16),
            vmem((NZ, peers, SLOTS, hidden), BF16),
            vmem((NZ, peers, SLOTS, hidden), BF16),
            vmem((count * top, BLK), F32),
            dma((4,)),
            dma((half * 2 * CHUNKS,)),
            dma((half * 2 * CHUNKS,)),
            dma((half * 2,)),
            dma((half * 2,)),
            dma((6,)),
            dma((6,)),
            dma((2,)),
            dma((NZ,)),
            dma((NZ,)),
            dma((NZ,)),
            dma((NZ,)),
            dma((NZ // batch,)),
            dma((NZ // batch,)),
            dma((NZ // batch,)),
        ],
        compiler_params=pltpu.CompilerParams(
            collective_id=0, has_side_effects=True, vmem_limit_bytes=VMEM_MIB * 1024 * 1024
        ),
        name="exchange",
    )(tokens, routes.T, weights, keep_mask, factor)
    return out.reshape(count, top, hidden)


def local(tokens, routes, weights, keep_mask, inv_factor):
    p, r, d = weights.shape[1:]
    return exchange(
        tokens, routes, weights.reshape(p * r, d), keep_mask.reshape(p * r, BLK), inv_factor.reshape(BLK, d)
    )


def solution(mesh):
    return jax.shard_map(
        local,
        mesh=mesh,
        in_specs=(
            P(("dp", "expert"), None),
            P(("dp", "expert"), None),
            P("expert", None, "dp", None),
            P("expert", None, "dp", None),
            P("expert", None, None),
        ),
        out_specs=P(("dp", "expert"), None, None),
        check_vma=False,
    )
```

time: 191 us -> 164 us (0.86)
  Pallas kernels: 187 us -> 161 us
    pallas_call x1, Pallas kernels: 178 us -> 161 us  [exchange(): pl.pallas_call(functools.partial(exchange_body, nx), out_shape=jax.ShapeD...]
    pallas_call x1 -> x0, Pallas kernels: 8.59 us -> none  [prune(): pl.pallas_call(prune_body, out_shape=jax.ShapeDtypeStruct((p * r, d), jnp...]
where the time goes in v2:
time: 164 us
  Pallas kernels  161 us (98%)
  local copies, waits for them, and re-layouts  2.36 us (1%)
    pallas_call x1, Pallas kernels, exchange(): pl.pallas_call(functools.partial(exchange_body, nx), out_shape=jax.ShapeD...  161 us

profile of v2, /device:TPU:1, one launch (start us, length us, event | category | flops | bytes accessed | tf_op | source)
XLA Modules:
  0.0 163.6 jit_solution(229566588946084184)
XLA Ops:
  0.0 161.3 %exchange.1 = bf16[768,768]{1,0:T(8,128)(2,1)} custom-call(bf16[96,2048]{1,0:T(8,128)(2,1)} %tok_in.1, s32[8,96]{1,0:T(8,128)} %bitcast.9, bf16[384,2048]{1,0:T(8,128)(2,1)} %bitcast.6, s32[384,128]{1,0:T(8,128)} %bitcast.8, f32[128,2048]{1,0:T(8,128)} %bitcast.7), custom_call_target="tpu_custom_call" | custom-call | tf_op jit(solution)/shard_map/exchange/pallas_call | solution.py:381
  161.3 2.4 %copy.7 = bf16[96,8,768]{2,1,0:T(8,128)(2,1)} copy(bf16[96,8,768]{2,1,0:T(8,128)(2,1)} %bitcast.5) | data formatting | bytes 2359296

commit v3 on v2

--- a/solution.py
+++ b/solution.py
@@ -20,8 +20,8 @@
 VMEM_MIB = 60
 FAR_MET = ()
 NY, NZ, NC = 4, 16, 2
-ORDER = (4, 5, 3, 6, 7, 8, 1, 2)
-EARLY = {7: (0,)}
+ORDER = (4, 1, 3, 5, 7, 8, 6, 2)
+EARLY = ((0, True), (1, False))
 
 
 def iota(shape, dim):
@@ -72,7 +72,7 @@
 
 
 def exchange_body(nx, tok_in, routes_in, weights_in, mask_in, factor_in, out, tok, weights, mask, factor, pruned,
-                  t_up, t_down, rt, packed, rows, whole, batch_rows, hid, back, home, code, load_s, ring_s, ring_r,
+                  t_up, t_down, rt, packed, rows, whole, batch_rows, hid, back, home, code, last_pick, load_s, ring_s, ring_r,
                   rt_s, rt_r, x_s, x_r, own_s, ys_s, ys_r, zs_s, zs_r, hs_s, hs_r, loc_s):
     tokens, width = tok.shape
     top = routes_in.shape[0]
@@ -254,7 +254,12 @@
             return pltpu.make_async_copy(hid.at[p], back.at[p], zs_r.at[p])
         return remote(hid.at[p], back.at[q], zs_s.at[p], zs_r.at[q], along_z(n))
 
-    def work(b):
+    def straight(n, q):
+        p, r = pos_of[n], pos_of[(NZ - n) % NZ]
+        device = {"expert": (((y + q // NC) % NY) * NZ + (z + n) % NZ) * NC + (c + q % NC) % NC}
+        return remote(hid.at[p, q], home.at[r, mirror(q)], zs_s.at[p], hs_r.at[r], device)
+
+    def multiply(b):
         first = b * batch
         if peers > 1:
             for k in range(batch):
@@ -268,8 +273,14 @@
             up = dot(batch_rows[...], whole[1, cols], ((1,), (1,)))
             value = gate / (1.0 + jnp.exp(-gate)) * up
             hid[pl.ds(first, batch), :, :, cols] = value.reshape(batch, peers, SLOTS, TILE).astype(BF16)
-        for n in sorted(order[first : first + batch], key=lambda n: -min(n, NZ - n)):
-            return_to(n).start()
+
+    def send_back(b):
+        for n in sorted(order[b * batch : (b + 1) * batch], key=lambda n: -min(n, NZ - n)):
+            if pos_of[n] < NZ - 2:
+                return_to(n).start()
+            else:
+                for q in range(peers):
+                    straight(n, q).start()
 
     def have_weights():
         for copy in own_copies:
@@ -278,14 +289,17 @@
             copy.wait_recv()
 
     jobs = {(1, 0): [lambda: pack_next(0, tok)], (1, 1): [find_code]}
-    for s in range(1, half):
+    for s in range(1, half if not EARLY else half - 1):
         jobs.setdefault((s + 1, 0), []).append(lambda s=s: pack_next(NZ - s, t_up.at[s]))
         jobs.setdefault((s + 1, 1), []).append(lambda s=s: pack_next(s, t_down.at[s]))
     jobs.setdefault((min(X_STEP, half), 2), []).append(forward_weights)
-    for s, early in EARLY.items():
-        jobs.setdefault((s, CHUNKS - 1), []).append(have_weights)
-        for b in early:
-            jobs[s, CHUNKS - 1].append(lambda b=b: work(b))
+    if EARLY:
+        last = jobs.setdefault((half - 1, CHUNKS - 1), [])
+        last += [hand_out, have_weights]
+        for b, send in EARLY:
+            last.append(lambda b=b: multiply(b))
+            if send:
+                last.append(lambda b=b: send_back(b))
     for s in range(1, half + 1):
         for h in range(CHUNKS):
             for way in range(2):
@@ -299,73 +313,89 @@
                         ring(way, s + 1, h).start()
             for job in jobs.get((s, h), []):
                 job()
+    for b, send in EARLY:
+        if not send:
+            send_back(b)
+    for n, block in (((NZ - half + 1, 0), (half - 1, 1)) if EARLY else ()):
+        pack_next(n, (t_up if block == 0 else t_down).at[n if block else NZ - n])
     pack_next(half, t_up.at[half])
     hand_out()
     if not EARLY:
         have_weights()
     for b in range(batches):
-        if not any(b in early for early in EARLY.values()):
-            work(b)
-
-    def homeward(b, q):
-        span = pl.ds(b * batch, batch)
-        return remote(back.at[span, q], home.at[span, mirror(q)], hs_s.at[b], hs_r.at[b], along_y(q))
-
-    def stay(b):
-        span = pl.ds(b * batch, batch)
-        return pltpu.make_async_copy(back.at[span, 0], home.at[span, 0], loc_s.at[b])
-
-    def send_home(b):
-        for k in range(batch):
-            block = back.at[b * batch + k]
-            pltpu.make_async_copy(block, block, zs_r.at[b * batch + k]).wait()
-        stay(b).start()
+        if b not in [early for early, _ in EARLY]:
+            multiply(b)
+            send_back(b)
+
+    def drain_outward():
+        for s in range(1, half + 1):
+            for way in range(2):
+                if names_has(way, s):
+                    names(way, s).wait_send()
+                for h in range(CHUNKS):
+                    if ring_has(way, s, h):
+                        ring(way, s, h).wait_send()
+        for copy in x_copies + x_forward:
+            copy.wait_send()
+        if peers > 1:
+            for p in range(NZ):
+                sent = packed.at[p, pl.ds(1, peers - 1)]
+                pltpu.make_async_copy(sent, sent, ys_s.at[p]).wait()
+
+    drain_outward()
+
+    def homeward(p, q):
+        return remote(back.at[p, q], home.at[p, mirror(q)], hs_s.at[p], hs_r.at[p], along_y(q))
+
+    def stay(p):
+        return pltpu.make_async_copy(back.at[p, 0], home.at[p, 0], loc_s.at[p])
+
+    def send_home(p):
+        pltpu.make_async_copy(back.at[p], back.at[p], zs_r.at[p]).wait()
         for q in range(1, peers):
-            homeward(b, q).start()
-
-    def unpack(b):
-        span = pl.ds(b * batch, batch)
-        stay(b).wait()
-        if peers > 1:
-            landed = home.at[span, pl.ds(1, peers - 1)]
-            pltpu.make_async_copy(landed, landed, hs_r.at[b]).wait()
-        count = batch * peers * SLOTS
-        values = home[span].astype(F32).reshape(count, out.shape[1]).astype(BF16)
+            homeward(p, q).start()
+        stay(p).start()
+
+    def picks(first, many):
         lanes = iota((slots_all, BLK), 1).astype(F32)
-        pick = [(code[...] == lanes + float(b * count + at)).astype(F32).astype(BF16) for at in range(0, count, BLK)]
-        pick = jnp.concatenate(pick, axis=1)[:, :count]
+        each = peers * SLOTS
+        made = [(code[...] == lanes + float(first * each + at)).astype(F32).astype(BF16) for at in range(0, many * each, BLK)]
+        return jnp.concatenate(made, axis=1)[:, : many * each]
+
+    def unpack(first, many, ready):
+        pick = last_pick[...] if ready else picks(first, many)
+        for p in range(first, first + many):
+            if ready:
+                pltpu.make_async_copy(home.at[p], home.at[p], hs_r.at[p]).wait()
+                continue
+            stay(p).wait()
+            if peers > 1:
+                landed = home.at[p, pl.ds(1, peers - 1)]
+                pltpu.make_async_copy(landed, landed, hs_r.at[p]).wait()
+        values = home[pl.ds(first, many)].astype(F32).reshape(many * peers * SLOTS, out.shape[1]).astype(BF16)
         for at in range(0, out.shape[1], TILE):
             cols = pl.ds(at, TILE)
             got = dot(pick, values[:, at : at + TILE], ((1,), (0,)))
-            if b > 0:
+            if first > 0:
                 got = out[:, cols].astype(F32) + got
             out[:, cols] = got.astype(BF16)
 
-    for b in range(batches):
-        send_home(b)
-        if b > 0:
-            unpack(b - 1)
-    unpack(batches - 1)
-
-    for s in range(1, half + 1):
-        for way in range(2):
-            if names_has(way, s):
-                names(way, s).wait_send()
-            for h in range(CHUNKS):
-                if ring_has(way, s, h):
-                    ring(way, s, h).wait_send()
-    for copy in x_copies + x_forward:
-        copy.wait_send()
+    groups = [(first, batch) for first in range(0, NZ - batch, batch)] + [(NZ - 4, 2), (NZ - 2, 2)]
+    for i, (first, many) in enumerate(groups):
+        for p in sorted(range(first, first + many), key=lambda p: -min(order[p], NZ - order[p])):
+            if p < NZ - 2:
+                send_home(p)
+        if i > 0:
+            unpack(*groups[i - 1], False)
+    last_pick[...] = picks(*groups[-1])
     for p in range(NZ):
-        if peers > 1:
-            sent = packed.at[p, pl.ds(1, peers - 1)]
-            pltpu.make_async_copy(sent, sent, ys_s.at[p]).wait()
         if order[p] != 0:
             pltpu.make_async_copy(hid.at[p], hid.at[p], zs_s.at[p]).wait()
+    unpack(NZ - 2, 2, True)
     if peers > 1:
-        for b in range(batches):
-            sent = back.at[pl.ds(b * batch, batch), pl.ds(1, peers - 1)]
-            pltpu.make_async_copy(sent, sent, hs_s.at[b]).wait()
+        for p in range(NZ - 2):
+            sent = back.at[p, pl.ds(1, peers - 1)]
+            pltpu.make_async_copy(sent, sent, hs_s.at[p]).wait()
 
 
 def exchange(tokens, routes, weights, keep_mask, factor):
@@ -406,6 +436,7 @@
             vmem((NZ, peers, SLOTS, hidden), BF16),
             vmem((NZ, peers, SLOTS, hidden), BF16),
             vmem((count * top, BLK), F32),
+            vmem((count * top, 2 * peers * SLOTS), BF16),
             dma((4,)),
             dma((half * 2 * CHUNKS,)),
             dma((half * 2 * CHUNKS,)),
@@ -418,9 +449,9 @@
             dma((NZ,)),
             dma((NZ,)),
             dma((NZ,)),
-            dma((NZ // batch,)),
-            dma((NZ // batch,)),
-            dma((NZ // batch,)),
+            dma((NZ,)),
+            dma((NZ,)),
+            dma((NZ,)),
         ],
         compiler_params=pltpu.CompilerParams(
             collective_id=0, has_side_effects=True, vmem_limit_bytes=VMEM_MIB * 1024 * 1024

time: 164 us -> 159 us (0.970)
  Pallas kernels: 161 us -> 156 us
    pallas_call x1, Pallas kernels: 161 us -> 156 us  [exchange(): pl.pallas_call(functools.partial(exchange_body, nx), out_shape=jax.ShapeD...]
where the time goes in v3:
time: 159 us; the launch traced here: 158 us
  Pallas kernels  156 us (98%)
  local copies, waits for them, and re-layouts  2.36 us (1%)
    pallas_call x1, Pallas kernels, exchange(): pl.pallas_call(functools.partial(exchange_body, nx), out_shape=jax.ShapeD...  156 us

profile of v3, /device:TPU:1, one launch (start us, length us, event | category | flops | bytes accessed | tf_op | source)
XLA Modules:
  0.0 158.5 jit_solution(2199525363636046166)
XLA Ops:
  0.0 156.1 %exchange.1 = bf16[768,768]{1,0:T(8,128)(2,1)} custom-call(bf16[96,2048]{1,0:T(8,128)(2,1)} %tok_in.1, s32[8,96]{1,0:T(8,128)} %bitcast.9, bf16[384,2048]{1,0:T(8,128)(2,1)} %bitcast.6, s32[384,128]{1,0:T(8,128)} %bitcast.8, f32[128,2048]{1,0:T(8,128)} %bitcast.7), custom_call_target="tpu_custom_call" | custom-call | tf_op jit(solution)/shard_map/exchange/pallas_call | solution.py:411
  156.1 2.4 %copy.7 = bf16[96,8,768]{2,1,0:T(8,128)(2,1)} copy(bf16[96,8,768]{2,1,0:T(8,128)(2,1)} %bitcast.5) | data formatting | bytes 2359296

commit v4 on v3

--- a/solution.py
+++ b/solution.py
@@ -16,6 +16,7 @@
 SLOTS = 8
 TILE = 256
 CHUNKS = 3
+FINISH_TILES = 2
 X_STEP = 3
 VMEM_MIB = 60
 FAR_MET = ()
@@ -71,9 +72,9 @@
         out_ref[:, at : at + step] = (w_ref[:, at : at + step].astype(F32) - upd).astype(out_ref.dtype)
 
 
-def exchange_body(nx, tok_in, routes_in, weights_in, mask_in, factor_in, out, tok, weights, mask, factor, pruned,
-                  t_up, t_down, rt, packed, rows, whole, batch_rows, hid, back, home, code, last_pick, load_s, ring_s, ring_r,
-                  rt_s, rt_r, x_s, x_r, own_s, ys_s, ys_r, zs_s, zs_r, hs_s, hs_r, loc_s):
+def exchange_body(nx, tok_in, routes_in, weights_in, mask_in, factor_in, out_hbm, pick_hbm, last_hbm, tok, weights, mask, factor, pruned,
+                  t_up, t_down, rt, packed, rows, whole, batch_rows, hid, back, home, code, out, last_pick, load_s, ring_s, ring_r,
+                  rt_s, rt_r, x_s, x_r, own_s, ys_s, ys_r, zs_s, zs_r, hs_s, hs_r, loc_s, out_s):
     tokens, width = tok.shape
     top = routes_in.shape[0]
     slots_all = tokens * top
@@ -254,10 +255,12 @@
             return pltpu.make_async_copy(hid.at[p], back.at[p], zs_r.at[p])
         return remote(hid.at[p], back.at[q], zs_s.at[p], zs_r.at[q], along_z(n))
 
+    relayed = NZ - batch
+
     def straight(n, q):
         p, r = pos_of[n], pos_of[(NZ - n) % NZ]
         device = {"expert": (((y + q // NC) % NY) * NZ + (z + n) % NZ) * NC + (c + q % NC) % NC}
-        return remote(hid.at[p, q], home.at[r, mirror(q)], zs_s.at[p], hs_r.at[r], device)
+        return remote(hid.at[p, q], last_hbm.at[r - relayed, mirror(q)], zs_s.at[p], hs_r.at[r], device)
 
     def multiply(b):
         first = b * batch
@@ -276,7 +279,7 @@
 
     def send_back(b):
         for n in sorted(order[b * batch : (b + 1) * batch], key=lambda n: -min(n, NZ - n)):
-            if pos_of[n] < NZ - 2:
+            if pos_of[n] < relayed:
                 return_to(n).start()
             else:
                 for q in range(peers):
@@ -362,17 +365,14 @@
         made = [(code[...] == lanes + float(first * each + at)).astype(F32).astype(BF16) for at in range(0, many * each, BLK)]
         return jnp.concatenate(made, axis=1)[:, : many * each]
 
-    def unpack(first, many, ready):
-        pick = last_pick[...] if ready else picks(first, many)
-        for p in range(first, first + many):
-            if ready:
-                pltpu.make_async_copy(home.at[p], home.at[p], hs_r.at[p]).wait()
-                continue
+    def unpack(first):
+        pick = picks(first, batch)
+        for p in range(first, first + batch):
             stay(p).wait()
             if peers > 1:
                 landed = home.at[p, pl.ds(1, peers - 1)]
                 pltpu.make_async_copy(landed, landed, hs_r.at[p]).wait()
-        values = home[pl.ds(first, many)].astype(F32).reshape(many * peers * SLOTS, out.shape[1]).astype(BF16)
+        values = flat(home[pl.ds(first, batch)])
         for at in range(0, out.shape[1], TILE):
             cols = pl.ds(at, TILE)
             got = dot(pick, values[:, at : at + TILE], ((1,), (0,)))
@@ -380,22 +380,54 @@
                 got = out[:, cols].astype(F32) + got
             out[:, cols] = got.astype(BF16)
 
-    groups = [(first, batch) for first in range(0, NZ - batch, batch)] + [(NZ - 4, 2), (NZ - 2, 2)]
-    for i, (first, many) in enumerate(groups):
-        for p in sorted(range(first, first + many), key=lambda p: -min(order[p], NZ - order[p])):
-            if p < NZ - 2:
-                send_home(p)
-        if i > 0:
-            unpack(*groups[i - 1], False)
-    last_pick[...] = picks(*groups[-1])
+    last_pick[...] = picks(relayed, batch)
+    pick_out = pltpu.make_async_copy(last_pick, pick_hbm, out_s.at[0])
+    pick_out.start()
+    for first in range(0, relayed, batch):
+        for p in sorted(range(first, first + batch), key=lambda p: -min(order[p], NZ - order[p])):
+            send_home(p)
+        if first > 0:
+            unpack(first - batch)
+    unpack(relayed - batch)
+    total_out = pltpu.make_async_copy(out, out_hbm, out_s.at[1])
+    total_out.start()
     for p in range(NZ):
         if order[p] != 0:
             pltpu.make_async_copy(hid.at[p], hid.at[p], zs_s.at[p]).wait()
-    unpack(NZ - 2, 2, True)
     if peers > 1:
-        for p in range(NZ - 2):
+        for p in range(relayed):
             sent = back.at[p, pl.ds(1, peers - 1)]
             pltpu.make_async_copy(sent, sent, hs_s.at[p]).wait()
+    pick_out.wait()
+    total_out.wait()
+    for k in range(batch):
+        pltpu.make_async_copy(last_hbm.at[k], last_hbm.at[k], hs_r.at[relayed + k]).wait()
+
+
+def flat(values):
+    return values.astype(F32).reshape(-1, values.shape[-1]).astype(BF16)
+
+
+def finish_body(partial, pick, last, out):
+    got = dot(pick[...], flat(last[...]), ((1,), (0,)))
+    out[...] = (partial[...].astype(F32) + got).astype(BF16)
+
+
+def finish(partial, pick, last):
+    rows, hidden = partial.shape
+    tile = rows // FINISH_TILES
+    return pl.pallas_call(
+        finish_body,
+        grid=(FINISH_TILES,),
+        out_shape=jax.ShapeDtypeStruct((rows, hidden), BF16),
+        in_specs=[
+            pl.BlockSpec((tile, hidden), lambda i: (i, 0)),
+            pl.BlockSpec((tile, pick.shape[1]), lambda i: (i, 0)),
+            pl.BlockSpec(last.shape, lambda i: (0, 0, 0, 0)),
+        ],
+        out_specs=pl.BlockSpec((tile, hidden), lambda i: (i, 0)),
+        name="finish",
+    )(partial, pick, last)
 
 
 def exchange(tokens, routes, weights, keep_mask, factor):
@@ -410,7 +442,11 @@
     vmem = pltpu.VMEM
     out = pl.pallas_call(
         functools.partial(exchange_body, nx),
-        out_shape=jax.ShapeDtypeStruct((count * top, hidden), BF16),
+        out_shape=[
+            jax.ShapeDtypeStruct((count * top, hidden), BF16),
+            jax.ShapeDtypeStruct((count * top, batch * peers * SLOTS), BF16),
+            jax.ShapeDtypeStruct((batch, peers, SLOTS, hidden), BF16),
+        ],
         in_specs=[
             pl.BlockSpec(memory_space=pltpu.HBM),
             pl.BlockSpec(memory_space=pltpu.VMEM),
@@ -418,7 +454,7 @@
             pl.BlockSpec(memory_space=pltpu.HBM),
             pl.BlockSpec(memory_space=pltpu.HBM),
         ],
-        out_specs=pl.BlockSpec(memory_space=pltpu.VMEM),
+        out_specs=[pl.BlockSpec(memory_space=pltpu.HBM)] * 3,
         scratch_shapes=[
             vmem((count, width), BF16),
             vmem((own, width), BF16),
@@ -436,7 +472,8 @@
             vmem((NZ, peers, SLOTS, hidden), BF16),
             vmem((NZ, peers, SLOTS, hidden), BF16),
             vmem((count * top, BLK), F32),
-            vmem((count * top, 2 * peers * SLOTS), BF16),
+            vmem((count * top, hidden), BF16),
+            vmem((count * top, batch * peers * SLOTS), BF16),
             dma((4,)),
             dma((half * 2 * CHUNKS,)),
             dma((half * 2 * CHUNKS,)),
@@ -452,13 +489,14 @@
             dma((NZ,)),
             dma((NZ,)),
             dma((NZ,)),
+            dma((2,)),
         ],
         compiler_params=pltpu.CompilerParams(
             collective_id=0, has_side_effects=True, vmem_limit_bytes=VMEM_MIB * 1024 * 1024
         ),
         name="exchange",
     )(tokens, routes.T, weights, keep_mask, factor)
-    return out.reshape(count, top, hidden)
+    return finish(*out).reshape(count, top, hidden)
 
 
 def local(tokens, routes, weights, keep_mask, inv_factor):

time: 159 us -> 157 us (0.987)
  local copies, waits for them, and re-layouts: 2.36 us -> 0 us
    unnamed x1 -> x0, local copies, waits for them, and re-layouts: 2.36 us -> none
    pallas_call x1 -> x2, Pallas kernels: 156 us -> 157 us  [the longest x1 154 us: exchange(): pl.pallas_call(functools.partial(exchange_body, nx), out_shape=[jax.Shape...]
where the time goes in v4:
time: 157 us
  Pallas kernels  157 us (100%)
    pallas_call x1, Pallas kernels, exchange(): pl.pallas_call(functools.partial(exchange_body, nx), out_shape=[jax.Shape...  154 us

profile of v4, /device:TPU:1, one launch (start us, length us, event | category | flops | bytes accessed | tf_op | source)
XLA Modules:
  0.0 157.0 jit_solution(15815044960239309818)
XLA Ops:
  0.0 154.3 %exchange.1 = (bf16[768,768]{1,0:T(8,128)(2,1)}, bf16[768,256]{1,0:T(8,128)(2,1)}, bf16[4,8,8,768]{3,2,1,0:T(8,128)(2,1)}) custom-call(bf16[96,2048]{1,0:T(8,128)(2,1)} %tok_in.1, s32[8,96]{1,0:T(8,128)} %bitcast.8, bf16[384,2048]{1,0:T(8,128)(2,1)} %bitcast.5, s32[384,128]{1,0:T(8,128)} %bitcast.7, f32[128,2048]{1,0:T(8,128)} %bitcast.6), custom_call_target="tpu_custom_call" | custom-call | tf_op jit(solution)/shard_map/exchange/pallas_call | solution.py:443
  154.3 2.7 %finish.1 = bf16[768,768]{1,0:T(8,128)(2,1)} custom-call(bf16[768,768]{1,0:T(8,128)(2,1)} %get-tuple-element.8.partial, bf16[768,256]{1,0:T(8,128)(2,1)} %get-tuple-element.9.pick, bf16[4,8,8,768]{3,2,1,0:T(8,128)(2,1)} %get-tuple-element.10.last), custom_call_target="tpu_custom_call" | custom-call | tf_op jit(solution)/shard_map/finish/pallas_call | solution.py:419

commit v5 on v4

--- a/solution.py
+++ b/solution.py
@@ -21,7 +21,7 @@
 VMEM_MIB = 60
 FAR_MET = ()
 NY, NZ, NC = 4, 16, 2
-ORDER = (4, 1, 3, 5, 7, 8, 6, 2)
+ORDER = (2, 1, 3, 5, 7, 8, 6, 4)
 EARLY = ((0, True), (1, False))
 
 

time: 157 us -> 156 us (level)
  no operation moved by 1% of the time
where the time goes in v5:
time: 156 us
  Pallas kernels  156 us (100%)
    pallas_call x1, Pallas kernels, exchange(): pl.pallas_call(functools.partial(exchange_body, nx), out_shape=[jax.Shape...  153 us

profile of v5, /device:TPU:1, one launch (start us, length us, event | category | flops | bytes accessed | tf_op | source)
XLA Modules:
  0.0 156.2 jit_solution(5541341887811598410)
XLA Ops:
  0.0 153.4 %exchange.1 = (bf16[768,768]{1,0:T(8,128)(2,1)}, bf16[768,256]{1,0:T(8,128)(2,1)}, bf16[4,8,8,768]{3,2,1,0:T(8,128)(2,1)}) custom-call(bf16[96,2048]{1,0:T(8,128)(2,1)} %tok_in.1, s32[8,96]{1,0:T(8,128)} %bitcast.8, bf16[384,2048]{1,0:T(8,128)(2,1)} %bitcast.5, s32[384,128]{1,0:T(8,128)} %bitcast.7, f32[128,2048]{1,0:T(8,128)} %bitcast.6), custom_call_target="tpu_custom_call" | custom-call | tf_op jit(solution)/shard_map/exchange/pallas_call | solution.py:443
  153.4 2.7 %finish.1 = bf16[768,768]{1,0:T(8,128)(2,1)} custom-call(bf16[768,768]{1,0:T(8,128)(2,1)} %get-tuple-element.8.partial, bf16[768,256]{1,0:T(8,128)(2,1)} %get-tuple-element.9.pick, bf16[4,8,8,768]{3,2,1,0:T(8,128)(2,1)} %get-tuple-element.10.last), custom_call_target="tpu_custom_call" | custom-call | tf_op jit(solution)/shard_map/finish/pallas_call | solution.py:419
